TPU v7x, 32 devices: a whole 2x2x4 slice. The times are simulated.
32 devices in a mesh: tm: 4 (over y, x), space: 8 (over z, core).
Axes of the slice: x: 2, y: 2, z: 4, core: 2. Of those that a mesh axis runs over, the one named last changes fastest.
Arguments:
- hidden_in: bfloat16 [8, 16, 32, 5120], P('tm', 'space'), may hold values from -6 to 6
- queries: bfloat16 [8, 16, 32, 5120], P('tm', 'space'), may hold values from -250 to 250
- keys: bfloat16 [8, 16, 32, 5120], P('tm', 'space'), may hold values from -250 to 250
- values: bfloat16 [8, 16, 32, 5120], P('tm', 'space'), may hold values from -6 to 6
- query_gain: float32 [5120], replicated, may hold values from 0.5 to 3
- key_gain: float32 [5120], replicated, may hold values from 0.5 to 3
- reach_time: int32 [40], replicated, may hold values from 0 to 1
- reach_rows: int32 [40], replicated, may hold values from 0 to 1
- reach_cols: int32 [40], replicated, may hold values from 0 to 2
- out_weight: bfloat16 [5120, 5120], P('space', 'tm'), may hold values from -0.25 to 0.25
- gate: float32 [5120], replicated, may hold values from -1.5 to 1.5
Outputs:
- output: bfloat16 [8, 16, 32, 5120], P('tm', 'space')
All inputs are finite; a program needn't handle non-finite values.
Results may differ from a plain program's by a relative error of at most 0.013.
The roundings to bfloat16 on the way count: a program that leaves them out, or rounds other values in their place, can miss the bound.
Values may be sent and summed in bfloat16 or wider, within the bound.
A program may use at most 128 MiB of HBM per device.

v0:
```python
import jax
import jax.numpy as jnp
from jax import lax
from jax.sharding import PartitionSpec as P

TW = 8


def passed_along(block, axis, distance):
    devices = range(lax.axis_size(axis))
    route = [(i - distance, i) for i in devices if i - distance in devices]
    return lax.ppermute(block, axis, route)


def normalize(source, gain):
    values_f = source.astype(jnp.float32)
    mean_square = jnp.mean(values_f * values_f, axis=-1, keepdims=True)
    return (values_f * lax.rsqrt(mean_square + 1e-06) * gain).astype(jnp.bfloat16)


def attend(
    query_block,
    key_region,
    value_region,
    first_frame,
    first_row,
    frame_count,
    row_count,
    reach_time,
    reach_rows,
    reach_cols,
):
    frames_here, rows_here, columns, inner = query_block.shape
    head_count = reach_time.shape[0]
    head_width = inner // head_count
    query_flat = query_block.reshape(-1, head_count, head_width)
    key_flat = key_region.reshape(-1, head_count, head_width)
    value_flat = value_region.reshape(-1, head_count, head_width)
    frame_q = first_frame + jnp.arange(frames_here, dtype=jnp.int32)
    frame_k = first_frame - 1 + jnp.arange(frames_here + 2, dtype=jnp.int32)
    row_q = first_row + jnp.arange(rows_here, dtype=jnp.int32)
    row_k = first_row - 1 + jnp.arange(rows_here + 2, dtype=jnp.int32)
    tiles = jnp.arange(columns, dtype=jnp.int32) // TW
    query_shape = (frames_here, rows_here, columns)
    key_shape = (frames_here + 2, rows_here + 2, columns)
    query_frame = jnp.broadcast_to(frame_q[:, None, None], query_shape).reshape(-1)
    query_row = jnp.broadcast_to(row_q[None, :, None], query_shape).reshape(-1)
    query_tile = jnp.broadcast_to(tiles[None, None, :], query_shape).reshape(-1)
    key_frame = jnp.broadcast_to(frame_k[:, None, None], key_shape).reshape(-1)
    key_row = jnp.broadcast_to(row_k[None, :, None], key_shape).reshape(-1)
    key_tile = jnp.broadcast_to(tiles[None, None, :], key_shape).reshape(-1)
    frame_gap = jnp.abs(query_frame[:, None] - key_frame[None, :])
    row_gap = jnp.abs(query_row[:, None] - key_row[None, :])
    tile_gap = jnp.abs(query_tile[:, None] - key_tile[None, :])
    inside = (key_frame >= 0) & (key_frame < frame_count) & (key_row >= 0) & (key_row < row_count)
    allowed = (frame_gap[None] <= reach_time[:, None, None]) & (
        row_gap[None] <= reach_rows[:, None, None]
    )
    allowed = allowed & (tile_gap[None] <= reach_cols[:, None, None]) & inside[None, None, :]
    scores = jnp.einsum(
        "qhd,khd->hqk", query_flat, key_flat, preferred_element_type=jnp.float32
    ) * head_width ** (-0.5)
    masked = jnp.where(allowed, scores, -jnp.inf)
    row_peak = jnp.max(masked, axis=2, keepdims=True)
    weights = jnp.exp(masked - row_peak)
    totals = jnp.sum(weights, axis=2, keepdims=True)
    rounded = weights.astype(jnp.bfloat16)
    mixed = jnp.einsum("hqk,khd->qhd", rounded, value_flat, preferred_element_type=jnp.float32)
    mixed = mixed / jnp.transpose(totals, (1, 0, 2))
    return mixed.reshape(mixed.shape[0], inner).astype(jnp.bfloat16)


def shards(
    hidden_in,
    queries,
    keys,
    values,
    query_gain,
    key_gain,
    reach_time,
    reach_rows,
    reach_cols,
    out_weight,
    gate,
):
    frames_here, rows_here, columns, inner = queries.shape
    width = hidden_in.shape[3]
    query_norm = normalize(queries, query_gain)
    key_norm = normalize(keys, key_gain)
    stacked = jnp.stack([key_norm, values])
    below_frame = passed_along(stacked[:, -1:], "tm", 1)
    above_frame = passed_along(stacked[:, :1], "tm", -1)
    framed = jnp.concatenate([below_frame, stacked, above_frame], axis=1)
    below_rows = passed_along(framed[:, :, -1:], "space", 1)
    above_rows = passed_along(framed[:, :, :1], "space", -1)
    region = jnp.concatenate([below_rows, framed, above_rows], axis=2)
    first_frame = lax.axis_index("tm") * frames_here
    first_row = lax.axis_index("space") * rows_here
    frame_count = frames_here * lax.axis_size("tm")
    row_count = rows_here * lax.axis_size("space")
    attention = attend(
        query_norm,
        region[0],
        region[1],
        first_frame,
        first_row,
        frame_count,
        row_count,
        reach_time,
        reach_rows,
        reach_cols,
    )
    token_count = attention.shape[0]
    gathered_rows = lax.all_gather(out_weight, "space", axis=0, tiled=True)
    group_terms = jnp.dot(
        lax.all_gather(attention, "tm", axis=0, tiled=True),
        gathered_rows,
        preferred_element_type=jnp.float32,
    )
    branch = lax.all_to_all(group_terms, "tm", split_axis=0, concat_axis=1, tiled=True)
    residual = hidden_in.reshape(token_count, width).astype(jnp.float32)
    output = (residual + gate * branch).astype(jnp.bfloat16)
    return output.reshape(frames_here, rows_here, columns, width)


def solution(mesh):
    in_specs = (
        P("tm", "space", None, None),
        P("tm", "space", None, None),
        P("tm", "space", None, None),
        P("tm", "space", None, None),
        P(),
        P(),
        P(),
        P(),
        P(),
        P("space", "tm"),
        P(),
    )
    out_specs = P("tm", "space", None, None)
    return jax.shard_map(shards, mesh=mesh, in_specs=in_specs, out_specs=out_specs, check_vma=False)
```

profile of v0, /device:TPU:0, one launch (start us, length us, event | category | flops | bytes accessed | tf_op | source)
XLA Modules:
  0.0 403.5 jit_solution(15969228863281141837)
XLA Ops:
  6.5 1.8 fusion.10
  8.3 1.7 fusion.22
  10.0 1.7 fusion.21
  11.8 5.9 %collective-permute-start = (bf16[2,1,2,32,5120]{4,3,2,1,0:T(8,128)(2,1)}, bf16[2,1,2,32,5120]{4,3,2,1,0:T(8,128)(2,1)}, u32[]{:S(2)}, u32[]{:S(2)}) collective-permute-start(bf16[2,1,2,32,5120]{4,3,2,1,0:T(8,128)(2,1)} %get-tuple-element.9), channel_id=1, source_target_pairs={{0,8},{8,16},{16,24},{1,9},{9,17},{17,25},{2,10},{10,18},{18,26},{... | collective-permute-start | bytes 3932168 | tf_op jit(solution)/shard_map/ppermute | solution.py:12
  17.7 1.3 collective-permute-start.1
  19.0 0.1 broadcast_in_dim.20
  19.1 0.1 sub.92
  19.2 0.1 broadcast_in_dim.19
  19.3 0.1 sub.89
  19.4 25.6 %collective-permute-done = bf16[2,1,2,32,5120]{4,3,2,1,0:T(8,128)(2,1)} collective-permute-done((bf16[2,1,2,32,5120]{4,3,2,1,0:T(8,128)(2,1)}, bf16[2,1,2,32,5120]{4,3,2,1,0:T(8,128)(2,1)}, u32[]{:S(2)}, u32[]{:S(2)}) %collective-permute-start) | collective-permute-done | bytes 1310752 | tf_op jit(solution)/shard_map/ppermute | solution.py:12
  45.0 30.0 %collective-permute-done.1 = bf16[2,1,2,32,5120]{4,3,2,1,0:T(8,128)(2,1)} collective-permute-done((bf16[2,1,2,32,5120]{4,3,2,1,0:T(8,128)(2,1)}, bf16[2,1,2,32,5120]{4,3,2,1,0:T(8,128)(2,1)}, u32[]{:S(2)}, u32[]{:S(2)}) %collective-permute-start.1) | collective-permute-done | bytes 1310752 | tf_op jit(solution)/shard_map/ppermute | solution.py:12
  75.0 2.8 pad_maximum_fusion.1
  77.8 0.0 copy-start.4
  77.8 2.8 fusion.25
  80.6 2.7 collective-permute-start.2
  83.4 1.3 collective-permute-start.3
  84.7 0.1 sub.98
  84.8 0.1 sub.96
  84.8 0.1 broadcast_in_dim.18
  84.9 0.1 sub.86
  85.0 0.1 broadcast_in_dim.17
  85.1 0.1 sub.83
  85.2 1.7 fusion.13
  86.9 1.7 fusion.15
  88.6 1.3 copy.20
  89.9 0.1 subtract_abs_fusion.2
  90.0 0.1 subtract_abs_fusion
  90.1 0.7 collective-permute-done.3
  90.9 8.9 %pad_maximum_fusion = bf16[2,4,4,32,5120]{4,3,2,1,0:T(8,128)(2,1)} fusion(bf16[2,4,1,32,5120]{4,3,2,1,0:T(8,128)(2,1)} %collective-permute-done.3, bf16[2,1,2,32,5120]{4,3,2,1,0:T(8,128)(2,1)} %collective-permute-done.1, bf16[1,2,2,32,5120]{4,3,2,1,0:T(8,128)(2,1)S(1)} %bitcast.35, bf16[1,2,2,32,5120]{4,3,2,1,0:T(8,128)(2,1)S(1)} %fusion.22, ...), kind=kLoop, calls=%fused_computation | loop fusion | flops 26214400 | bytes 20971520 | tf_op jit(solution)/shard_map/concatenate | solution.py:96
  99.8 9.1 %fusion.24 = (bf16[1,4,4,32,5120]{4,3,2,1,0:T(8,128)(2,1)}, bf16[1,4,4,32,5120]{4,3,2,1,0:T(8,128)(2,1)}) fusion(bf16[2,4,4,32,5120]{4,3,2,1,0:T(8,128)(2,1)} %pad_maximum_fusion), kind=kLoop, calls=%fused_computation.44 | loop fusion | bytes 20971520 | tf_op jit(solution)/shard_map/slice | solution.py:104
  108.9 4.1 %copy.21 = bf16[64,8,40,128]{3,2,1,0:T(8,128)(2,1)S(1)} copy(bf16[64,8,40,128]{3,1,2,0:T(8,128)(2,1)} %bitcast.32) | data formatting | bytes 10485760
  113.0 0.0 copy-start.2
  113.0 0.0 copy-start.8
  113.0 1.4 copy.19
  114.5 4.7 %fusion.26 = (f32[40,128]{1,0:T(8,128)S(1)}, f32[40,128,512]{2,1,0:T(8,128)S(1)}) fusion(bf16[512,40,128]{2,1,0:T(8,128)(2,1)S(1)} %bitcast.38, bf16[128,40,128]{2,1,0:T(8,128)(2,1)S(1)} %bitcast.41, pred[512]{0:T(512)(128)(4,1)S(1)} %compare_and_fusion, s32[40]{0:T(128)S(1)} %copy-done.6, s32[128,512]{1,0:T(8,128)S(1)} %get-tuple-element.13, ...), kind=kOutput, calls=%fused_computation.46 | convolution fusion | flops 694676480 | bytes 17847264 | tf_op jit(solution)/shard_map/qhd,khd->hqk/dot_general | solution.py:60
  119.2 2.4 fusion
  121.7 1.5 copy-done.1
  123.2 7.1 %fusion.16 = bf16[128,40,128]{0,2,1:T(8,128)(2,1)} fusion(f32[40,128,512]{2,1,0:T(8,128)} %copy-done.1, f32[40,128]{1,0:T(8,128)S(1)} %get-tuple-element.11, bf16[512,40,128]{2,1,0:T(8,128)(2,1)S(1)} %bitcast.37, f32[128,40]{0,1:T(8,128)S(1)} %bitcast.43), kind=kOutput, calls=%fused_computation.24 | convolution fusion | flops 677642240 | bytes 17080320 | tf_op jit(solution)/shard_map/hqk,khd->qhd/dot_general | solution.py:68
  130.3 0.0 all-gather.3.cloned.1.call-update
  130.3 0.0 all-gather.5.cloned.1.call-start
  130.3 0.7 all-gather.5.cloned.1.call-update
  131.1 86.1 %all-gather.3.cloned.1.call-done = bf16[512,5120]{0,1:T(8,128)(2,1)} async-done(((bf16[128,5120]{0,1:T(8,128)(2,1)}), bf16[512,5120]{0,1:T(8,128)(2,1)}) %all-gather.3.cloned.1.call-update) | async-done | bytes 5242896 | tf_op jit(solution)/shard_map/all_gather | solution.py:116
  217.2 122.7 %all-gather.5.cloned.1.call-done = bf16[5120,1280]{1,0:T(8,128)(2,1)} async-done(((bf16[640,1280]{1,0:T(8,128)(2,1)}), bf16[5120,1280]{1,0:T(8,128)(2,1)}) %all-gather.5.cloned.1.call-update) | async-done | bytes 13107216 | tf_op jit(solution)/shard_map/all_gather | solution.py:114
  339.9 11.5 %fusion.27 = f32[512,1280]{1,0:T(8,128)S(1)} fusion(bf16[512,5120]{0,1:T(8,128)(2,1)} %all-gather.3.cloned.1.call-done, bf16[5120,1280]{1,0:T(8,128)(2,1)} %all-gather.5.cloned.1.call-done), kind=kOutput, calls=%fused_computation.47 | convolution fusion | flops 6710886400 | bytes 20971520 | tf_op jit(solution)/shard_map/dot_general | solution.py:115
  351.4 34.9 %all_to_all.19 = f32[4,128,1280]{2,1,0:T(8,128)S(1)} all-to-all(f32[4,128,1280]{2,1,0:T(8,128)S(1)} %bitcast.40), channel_id=1, replica_groups=mesh['tm'=4,'space'=8] {'tm'}, dimensions={0} | all-to-all | bytes 5242880 | tf_op jit(solution)/shard_map/all_to_all | solution.py:120
  386.2 3.2 copy.18
  389.4 4.1 %all_to_all.17 = f32[2,2,32,5120]{3,2,1,0:T(8,128)} reshape(f32[128,4,1280]{2,1,0:T(4,128)} %copy.18) | data formatting | bytes 5242880 | tf_op jit(solution)/shard_map/all_to_all | solution.py:120
  393.5 3.1 add_convert_fusion
  (31 shorter events, 0.1 us)
Async XLA Ops:
  6.5 3.5 copy-start
  6.5 210.6 %all-gather.3.cloned.1.call-start = ((), (), s32[]{:S(2)}) async-start(), calls=%async_computation.1 | async-start | bytes 6553600 | tf_op jit(solution)/shard_map/all_gather | solution.py:116
  11.8 33.2 %collective-permute-start = (bf16[2,1,2,32,5120]{4,3,2,1,0:T(8,128)(2,1)}, bf16[2,1,2,32,5120]{4,3,2,1,0:T(8,128)(2,1)}, u32[]{:S(2)}, u32[]{:S(2)}) collective-permute-start(bf16[2,1,2,32,5120]{4,3,2,1,0:T(8,128)(2,1)} %get-tuple-element.9), channel_id=1, source_target_pairs={{0,8},{8,16},{16,24},{1,9},{9,17},{17,25},{2,10},{10,18},{18,26},{... | collective-permute-start | bytes 3932168 | tf_op jit(solution)/shard_map/ppermute | solution.py:12
  17.7 57.3 %collective-permute-start.1 = (bf16[2,1,2,32,5120]{4,3,2,1,0:T(8,128)(2,1)}, bf16[2,1,2,32,5120]{4,3,2,1,0:T(8,128)(2,1)}, u32[]{:S(2)}, u32[]{:S(2)}) collective-permute-start(bf16[2,1,2,32,5120]{4,3,2,1,0:T(8,128)(2,1)} %get-tuple-element.10), channel_id=1, source_target_pairs={{8,0},{16,8},{24,16},{9,1},{17,9},{25,17},{10,2},{18,10},{26,18},{... | collective-permute-start | bytes 3932168 | tf_op jit(solution)/shard_map/ppermute | solution.py:12
  77.8 9.0 %copy-start.4 = (f32[5120]{0:T(1024)S(1)}, f32[5120]{0:T(1024)}, u32[]{:S(2)}) copy-start(f32[5120]{0:T(1024)} %param.15) | copy-start | bytes 61444
  80.6 9.5 %collective-permute-start.2 = (bf16[2,4,1,32,5120]{4,3,2,1,0:T(8,128)(2,1)}, bf16[2,4,1,32,5120]{4,3,2,1,0:T(8,128)(2,1)}, u32[]{:S(2)}, u32[]{:S(2)}) collective-permute-start(bf16[2,4,1,32,5120]{4,3,2,1,0:T(8,128)(2,1)} %get-tuple-element.7), channel_id=1, source_target_pairs={{0,1},{1,2},{2,3},{3,4},{4,5},{5,6},{6,7},{8,9},{9,10},{10,11},{11... | collective-permute-start | bytes 7864328 | tf_op jit(solution)/shard_map/ppermute | solution.py:12
  83.4 7.5 %collective-permute-start.3 = (bf16[2,4,1,32,5120]{4,3,2,1,0:T(8,128)(2,1)}, bf16[2,4,1,32,5120]{4,3,2,1,0:T(8,128)(2,1)}, u32[]{:S(2)}, u32[]{:S(2)}) collective-permute-start(bf16[2,4,1,32,5120]{4,3,2,1,0:T(8,128)(2,1)} %get-tuple-element.8), channel_id=1, source_target_pairs={{1,0},{2,1},{3,2},{4,3},{5,4},{6,5},{7,6},{9,8},{10,9},{11,10},{12... | collective-permute-start | bytes 7864328 | tf_op jit(solution)/shard_map/ppermute | solution.py:12
  108.9 4.1 %slice-start = ((s8[5242880]{0:T(1024)(128)(4,1)}), s8[4194304]{0:T(1024)(128)(4,1)S(1)}, s32[]{:S(2)}) async-start(s8[5242880]{0:T(1024)(128)(4,1)} %bitcast.29), calls=%async_computation.3 | async-start | bytes 8388608
  108.9 4.1 %slice-start.1 = ((s8[5242880]{0:T(1024)(128)(4,1)}), s8[1048576]{0:T(1024)(128)(4,1)S(1)}, s32[]{:S(2)}) async-start(s8[5242880]{0:T(1024)(128)(4,1)} %bitcast.29), calls=%async_computation.4 | async-start | bytes 2097152
  113.0 1.5 copy-start.2
  113.0 1.5 copy-start.6
  113.0 1.5 copy-start.7
  113.0 1.5 copy-start.8
  119.2 4.0 copy-start.1
  130.3 209.6 %all-gather.5.cloned.1.call-start = ((), (), s32[]{:S(2)}) async-start(), calls=%async_computation.2 | async-start | bytes 14745600 | tf_op jit(solution)/shard_map/all_gather | solution.py:114
  389.4 4.1 %copy-start.3 = (bf16[2,2,32,5120]{3,2,1,0:T(8,128)(2,1)S(1)}, bf16[2,2,32,5120]{3,2,1,0:T(8,128)(2,1)}, u32[]{:S(2)}) copy-start(bf16[2,2,32,5120]{3,2,1,0:T(8,128)(2,1)} %param.11) | copy-start | bytes 3932164
  389.4 4.1 %copy-start.5 = (f32[5120]{0:T(1024)S(1)}, f32[5120]{0:T(1024)}, u32[]{:S(2)}) copy-start(f32[5120]{0:T(1024)} %param.21) | copy-start | bytes 61444
Sparse Core Ops, SparseCore 0:
  130.4 86.7 all-gather.2
  218.8 120.9 all-gather.4
where the time goes:
time: 404 us
  waiting for transfers between devices  266 us (66%)
  blocking collectives  34.9 us (9%)
  local copies, waits for them, and re-layouts  28.3 us (7%)
  other arithmetic  26.2 us (6%)
  matrix products  23.3 us (6%)
  between operations  13.7 us (3%)
  starting transfers between devices  11.3 us (3%)
    all_gather x1, waiting for transfers between devices, shards(): gathered_rows = lax.all_gather(out_weight, 'space', axis=0, tiled=True)  123 us
    all_gather x1, waiting for transfers between devices, shards(): lax.all_gather(attention, 'tm', axis=0, tiled=True)  86.1 us
    ppermute x4, waiting for transfers between devices, passed_along(): return lax.ppermute(block, axis, route)  56.4 us
    all_to_all x1, blocking collectives, shards(): lax.all_to_all(group_terms, 'tm', split_axis=0, concat_axis=1, tiled=True)  34.9 us
    dot_general x1, matrix products, shards(): jnp.dot(lax.all_gather(attention, 'tm', axis=0, tiled=True), gathered_row...  11.5 us
    ppermute x4, starting transfers between devices, passed_along(): return lax.ppermute(block, axis, route)  11.3 us
    slice x1, local copies, waits for them, and re-layouts, shards(): region[1]  9.06 us
    concatenate x1, other arithmetic, shards(): region = jnp.concatenate([below_rows, framed, above_rows], axis=2)  8.94 us
  transfers between devices with their start and end apart: 6, of which 5 were waited for; matrix products, arithmetic and copies ran while one was open for 1% of the time, Pallas kernels for 0%

commit v1 on v0

--- a/solution.py
+++ b/solution.py
@@ -111,7 +111,14 @@
         reach_cols,
     )
     token_count = attention.shape[0]
-    gathered_rows = lax.all_gather(out_weight, "space", axis=0, tiled=True)
+    ring = [out_weight]
+    for hop in range(7):
+        ring.append(lax.ppermute(ring[-1], "space", [(dev, (dev + 1) % 8) for dev in range(8)]))
+    gathered_rows = jnp.roll(
+        jnp.concatenate(ring[::-1], axis=0),
+        (lax.axis_index("space") + 1) * ring[0].shape[0],
+        axis=0,
+    )
     group_terms = jnp.dot(
         lax.all_gather(attention, "tm", axis=0, tiled=True),
         gathered_rows,

time: 404 us -> 332 us (0.82)
  waiting for transfers between devices: 266 us -> 158 us
  local copies, waits for them, and re-layouts: 28.3 us -> 65.6 us
  blocking collectives: 34.9 us -> 25.9 us
    all_gather x1 -> x0, waiting for transfers between devices: 123 us -> none  [shards(): gathered_rows = lax.all_gather(out_weight, 'space', axis=0, tiled=True)]
    ppermute x0 -> x7, waiting for transfers between devices: none -> 102 us  [shards(): lax.ppermute(ring[-1], 'space', [(dev, (dev + 1) % 8) for dev in range(8)])]
    all_gather x1, waiting for transfers between devices: 86.1 us -> 0.01 us  [shards(): lax.all_gather(attention, 'tm', axis=0, tiled=True)]
    unnamed x25 -> x36, local copies, waits for them, and re-layouts: 8.41 us -> 46 us
    all_to_all x1, blocking collectives: 34.9 us -> 25.9 us  [shards(): lax.all_to_all(group_terms, 'tm', split_axis=0, concat_axis=1, tiled=True)]
  transfers between devices with their start and end apart: 6 -> 12, of which waited for: 5 -> 7; matrix products, arithmetic and copies ran while one was open for 1% -> 28% of each run, Pallas kernels for 0% -> 0%
where the time goes in v1:
time: 332 us; the launch traced here: 331 us
  waiting for transfers between devices  158 us (48%)
  local copies, waits for them, and re-layouts  65.6 us (20%)
  other arithmetic  27.8 us (8%)
  matrix products  26 us (8%)
  blocking collectives  25.9 us (8%)
  starting transfers between devices  13.9 us (4%)
  between operations  13.6 us (4%)
    ppermute x7, waiting for transfers between devices, shards(): lax.ppermute(ring[-1], 'space', [(dev, (dev + 1) % 8) for dev in range(8)])  102 us
    ppermute x4, waiting for transfers between devices, passed_along(): return lax.ppermute(block, axis, route)  55.6 us
    unnamed x36, local copies, waits for them, and re-layouts  46 us
    all_to_all x1, blocking collectives, shards(): lax.all_to_all(group_terms, 'tm', split_axis=0, concat_axis=1, tiled=True)  25.9 us
    ppermute x4, starting transfers between devices, passed_along(): return lax.ppermute(block, axis, route)  13.5 us
    dot_general x1, matrix products, shards(): jnp.dot(lax.all_gather(attention, 'tm', axis=0, tiled=True), gathered_row...  11.5 us
    dot_general x1, matrix products, attend(): jnp.einsum('hqk,khd->qhd', rounded, value_flat, preferred_element_type=jn...  9.79 us
    slice x1, local copies, waits for them, and re-layouts, shards(): region[1]  9.06 us
  transfers between devices with their start and end apart: 12, of which 7 were waited for; matrix products, arithmetic and copies ran while one was open for 28% of the time, Pallas kernels for 0%

profile of v1, /device:TPU:0, one launch (start us, length us, event | category | flops | bytes accessed | tf_op | source)
XLA Modules:
  0.0 331.0 jit_solution(7820716988760322531)
XLA Ops:
  6.5 1.8 fusion.12
  8.3 1.7 fusion.24
  10.0 3.0 fusion.23
  13.1 5.9 %collective-permute-start = (bf16[2,1,2,32,5120]{4,3,2,1,0:T(8,128)(2,1)}, bf16[2,1,2,32,5120]{4,3,2,1,0:T(8,128)(2,1)}, u32[]{:S(2)}, u32[]{:S(2)}) collective-permute-start(bf16[2,1,2,32,5120]{4,3,2,1,0:T(8,128)(2,1)} %get-tuple-element.9), channel_id=1, source_target_pairs={{0,8},{8,16},{16,24},{1,9},{9,17},{17,25},{2,10},{10,18},{18,26},{... | collective-permute-start | bytes 3932168 | tf_op jit(solution)/shard_map/ppermute | solution.py:12
  19.0 1.3 collective-permute-start.1
  20.7 25.6 %collective-permute-done = bf16[2,1,2,32,5120]{4,3,2,1,0:T(8,128)(2,1)} collective-permute-done((bf16[2,1,2,32,5120]{4,3,2,1,0:T(8,128)(2,1)}, bf16[2,1,2,32,5120]{4,3,2,1,0:T(8,128)(2,1)}, u32[]{:S(2)}, u32[]{:S(2)}) %collective-permute-start) | collective-permute-done | bytes 1310752 | tf_op jit(solution)/shard_map/ppermute | solution.py:12
  46.3 30.0 %collective-permute-done.1 = bf16[2,1,2,32,5120]{4,3,2,1,0:T(8,128)(2,1)} collective-permute-done((bf16[2,1,2,32,5120]{4,3,2,1,0:T(8,128)(2,1)}, bf16[2,1,2,32,5120]{4,3,2,1,0:T(8,128)(2,1)}, u32[]{:S(2)}, u32[]{:S(2)}) %collective-permute-start.1) | collective-permute-done | bytes 1310752 | tf_op jit(solution)/shard_map/ppermute | solution.py:12
  76.3 2.8 pad_maximum_fusion.1
  79.2 2.8 fusion.28
  82.0 5.0 %collective-permute-start.2 = (bf16[2,4,1,32,5120]{4,3,2,1,0:T(8,128)(2,1)}, bf16[2,4,1,32,5120]{4,3,2,1,0:T(8,128)(2,1)}, u32[]{:S(2)}, u32[]{:S(2)}) collective-permute-start(bf16[2,4,1,32,5120]{4,3,2,1,0:T(8,128)(2,1)} %get-tuple-element.7), channel_id=1, source_target_pairs={{0,1},{1,2},{2,3},{3,4},{4,5},{5,6},{6,7},{8,9},{9,10},{10,11},{11... | collective-permute-start | bytes 7864328 | tf_op jit(solution)/shard_map/ppermute | solution.py:12
  87.0 1.3 collective-permute-start.3
  88.8 1.7 fusion.15
  90.5 20.2 %collective-permute-done.5 = bf16[640,1280]{1,0:T(8,128)(2,1)} collective-permute-done((bf16[640,1280]{1,0:T(8,128)(2,1)}, bf16[640,1280]{1,0:T(8,128)(2,1)}, u32[]{:S(2)}, u32[]{:S(2)}) %collective-permute-start.5) | collective-permute-done | bytes 1638432 | tf_op jit(solution)/shard_map/ppermute | solution.py:116
  110.7 1.7 fusion.17
  112.5 1.3 copy.20
  114.0 33.5 %collective-permute-done.6 = bf16[640,1280]{1,0:T(8,128)(2,1)} collective-permute-done((bf16[640,1280]{1,0:T(8,128)(2,1)}, bf16[640,1280]{1,0:T(8,128)(2,1)}, u32[]{:S(2)}, u32[]{:S(2)}) %collective-permute-start.6) | collective-permute-done | bytes 1638432 | tf_op jit(solution)/shard_map/ppermute | solution.py:116
  147.5 9.0 %pad_maximum_fusion = bf16[2,4,4,32,5120]{4,3,2,1,0:T(8,128)(2,1)} fusion(bf16[2,4,1,32,5120]{4,3,2,1,0:T(8,128)(2,1)} %collective-permute-done.3, bf16[2,1,2,32,5120]{4,3,2,1,0:T(8,128)(2,1)} %collective-permute-done.1, bf16[1,2,2,32,5120]{4,3,2,1,0:T(8,128)(2,1)S(1)} %bitcast.32, bf16[1,2,2,32,5120]{4,3,2,1,0:T(8,128)(2,1)S(1)} %fusion.24, ...), kind=kLoop, calls=%fused_computation.2 | loop fusion | flops 26214400 | bytes 20971520 | tf_op jit(solution)/shard_map/concatenate | solution.py:96
  156.5 9.1 %fusion.27 = (bf16[1,4,4,32,5120]{4,3,2,1,0:T(8,128)(2,1)}, bf16[1,4,4,32,5120]{4,3,2,1,0:T(8,128)(2,1)}) fusion(bf16[2,4,4,32,5120]{4,3,2,1,0:T(8,128)(2,1)} %pad_maximum_fusion), kind=kLoop, calls=%fused_computation.63 | loop fusion | bytes 20971520 | tf_op jit(solution)/shard_map/slice | solution.py:104
  165.5 6.4 %copy.19 = bf16[64,8,40,128]{3,2,1,0:T(8,128)(2,1)} copy(bf16[64,8,40,128]{3,1,2,0:T(8,128)(2,1)} %bitcast.29) | data formatting | bytes 10485760
  172.0 1.4 copy.21
  173.7 4.7 %fusion.29 = (f32[40,128]{1,0:T(8,128)S(1)}, f32[40,128,512]{2,1,0:T(8,128)S(1)}) fusion(bf16[512,40,128]{2,1,0:T(8,128)(2,1)S(1)} %bitcast.35, bf16[128,40,128]{2,1,0:T(8,128)(2,1)S(1)} %bitcast.39, pred[512]{0:T(512)(128)(4,1)S(1)} %compare_and_fusion, s32[40]{0:T(128)S(1)} %copy-done.6, s32[128,512]{1,0:T(8,128)S(1)} %get-tuple-element.13, ...), kind=kOutput, calls=%fused_computation.65 | convolution fusion | flops 694676480 | bytes 17847264 | tf_op jit(solution)/shard_map/qhd,khd->hqk/dot_general | solution.py:60
  178.5 2.4 fusion.2
  180.9 1.5 copy-done.2
  182.4 13.8 %collective-permute-done.8 = bf16[640,1280]{1,0:T(8,128)(2,1)S(1)} collective-permute-done((bf16[640,1280]{1,0:T(8,128)(2,1)}, bf16[640,1280]{1,0:T(8,128)(2,1)S(1)}, u32[]{:S(2)}, u32[]{:S(2)}) %collective-permute-start.8) | collective-permute-done | bytes 1638432 | tf_op jit(solution)/shard_map/ppermute | solution.py:116
  196.2 9.8 %fusion.18 = bf16[128,40,128]{0,2,1:T(8,128)(2,1)} fusion(f32[40,128,512]{2,1,0:T(8,128)} %copy-done.2, f32[40,128]{1,0:T(8,128)S(1)} %get-tuple-element.11, bf16[512,40,128]{2,1,0:T(8,128)(2,1)} %bitcast.34, f32[128,40]{0,1:T(8,128)S(1)} %bitcast.40), kind=kOutput, calls=%fused_computation.26 | convolution fusion | flops 677642240 | bytes 17080320 | tf_op jit(solution)/shard_map/hqk,khd->qhd/dot_general | solution.py:68
  206.0 12.5 %collective-permute-done.9 = bf16[640,1280]{1,0:T(8,128)(2,1)S(1)} collective-permute-done((bf16[640,1280]{1,0:T(8,128)(2,1)S(1)}, bf16[640,1280]{1,0:T(8,128)(2,1)S(1)}, u32[]{:S(2)}, u32[]{:S(2)}) %collective-permute-start.9) | collective-permute-done | bytes 1638432 | tf_op jit(solution)/shard_map/ppermute | solution.py:116
  218.6 22.4 %collective-permute-done.10 = bf16[640,1280]{1,0:T(8,128)(2,1)} collective-permute-done((bf16[640,1280]{1,0:T(8,128)(2,1)S(1)}, bf16[640,1280]{1,0:T(8,128)(2,1)}, u32[]{:S(2)}, u32[]{:S(2)}) %collective-permute-start.10) | collective-permute-done | bytes 1638432 | tf_op jit(solution)/shard_map/ppermute | solution.py:116
  241.0 2.8 constant_dynamic-update-slice_fusion.15
  243.8 1.3 constant_dynamic-update-slice_fusion.14
  245.1 1.3 constant_dynamic-update-slice_fusion.13
  246.4 2.8 constant_dynamic-update-slice_fusion.12
  249.2 2.7 constant_dynamic-update-slice_fusion.11
  251.9 2.8 constant_dynamic-update-slice_fusion.10
  254.6 2.7 constant_dynamic-update-slice_fusion.9
  257.4 2.8 constant_dynamic-update-slice_fusion.8
  260.2 2.7 constant_dynamic-update-slice_fusion.7
  262.9 1.3 constant_dynamic-update-slice_fusion.6
  264.1 1.3 constant_dynamic-update-slice_fusion.5
  265.4 2.7 constant_dynamic-update-slice_fusion.4
  268.1 2.7 constant_dynamic-update-slice_fusion.3
  270.9 2.7 constant_dynamic-update-slice_fusion.2
  273.6 2.7 constant_dynamic-update-slice_fusion.1
  276.3 2.8 constant_dynamic-update-slice_fusion
  279.1 11.5 %fusion = f32[512,1280]{1,0:T(8,128)S(1)} fusion(bf16[512,5120]{0,1:T(8,128)(2,1)} %all-gather.2.cloned.1.call-done, bf16[10240,1280]{1,0:T(8,128)(2,1)} %constant_dynamic-update-slice_fusion, s32[]{:T(128)S(6)} %select_n.29), kind=kOutput, calls=%fused_computation | convolution fusion | flops 6710886400 | bytes 20971524 | tf_op jit(solution)/shard_map/dot_general | solution.py:122
  290.6 25.9 %all_to_all.19 = f32[4,128,1280]{2,1,0:T(8,128)S(1)} all-to-all(f32[4,128,1280]{2,1,0:T(8,128)S(1)} %bitcast.37), channel_id=1, replica_groups=mesh['tm'=4,'space'=8] {'tm'}, dimensions={0} | all-to-all | bytes 5242880 | tf_op jit(solution)/shard_map/all_to_all | solution.py:127
  316.5 1.7 copy.18
  318.2 2.5 all_to_all.17
  320.7 3.5 %add_convert_fusion = bf16[2,2,32,5120]{3,2,1,0:T(8,128)(2,1)} fusion(f32[2,2,32,5120]{3,2,1,0:T(8,128)} %all_to_all.17, bf16[2,2,32,5120]{3,2,1,0:T(8,128)(2,1)} %param.11, f32[5120]{0:T(1024)S(1)} %copy-done.5), kind=kLoop, calls=%fused_computation.27 | loop fusion | flops 2621440 | bytes 5263360 | tf_op jit(solution)/shard_map/convert_element_type | solution.py:129
  (53 shorter events, 1.5 us)
Async XLA Ops:
  6.5 69.8 %copy-start.1 = (bf16[2,2,32,5120]{3,2,1,0:T(8,128)(2,1)S(1)}, bf16[2,2,32,5120]{3,2,1,0:T(8,128)(2,1)}, u32[]{:S(2)}) copy-start(bf16[2,2,32,5120]{3,2,1,0:T(8,128)(2,1)} %param.14) | copy-start | bytes 3932164
  6.5 272.5 %all-gather.2.cloned.1.call-start = ((), (), s32[]{:S(2)}) async-start(), calls=%async_computation.1 | async-start | bytes 6553600 | tf_op jit(solution)/shard_map/all_gather | solution.py:123
  13.1 33.2 %collective-permute-start = (bf16[2,1,2,32,5120]{4,3,2,1,0:T(8,128)(2,1)}, bf16[2,1,2,32,5120]{4,3,2,1,0:T(8,128)(2,1)}, u32[]{:S(2)}, u32[]{:S(2)}) collective-permute-start(bf16[2,1,2,32,5120]{4,3,2,1,0:T(8,128)(2,1)} %get-tuple-element.9), channel_id=1, source_target_pairs={{0,8},{8,16},{16,24},{1,9},{9,17},{17,25},{2,10},{10,18},{18,26},{... | collective-permute-start | bytes 3932168 | tf_op jit(solution)/shard_map/ppermute | solution.py:12
  19.0 57.3 %collective-permute-start.1 = (bf16[2,1,2,32,5120]{4,3,2,1,0:T(8,128)(2,1)}, bf16[2,1,2,32,5120]{4,3,2,1,0:T(8,128)(2,1)}, u32[]{:S(2)}, u32[]{:S(2)}) collective-permute-start(bf16[2,1,2,32,5120]{4,3,2,1,0:T(8,128)(2,1)} %get-tuple-element.10), channel_id=1, source_target_pairs={{8,0},{16,8},{24,16},{9,1},{17,9},{25,17},{10,2},{18,10},{26,18},{... | collective-permute-start | bytes 3932168 | tf_op jit(solution)/shard_map/ppermute | solution.py:12
  20.3 58.8 %collective-permute-start.4 = (bf16[640,1280]{1,0:T(8,128)(2,1)}, bf16[640,1280]{1,0:T(8,128)(2,1)}, u32[]{:S(2)}, u32[]{:S(2)}) collective-permute-start(bf16[640,1280]{1,0:T(8,128)(2,1)} %param.20), channel_id=1, source_target_pairs={{0,1},{1,2},{2,3},{3,4},{4,5},{5,6},{6,7},{7,0},{8,9},{9,10},{10,1... | collective-permute-start | bytes 4915208 | tf_op jit(solution)/shard_map/ppermute | solution.py:116
  79.1 31.6 %copy-start.4 = (f32[5120]{0:T(1024)S(1)}, f32[5120]{0:T(1024)}, u32[]{:S(2)}) copy-start(f32[5120]{0:T(1024)} %param.15) | copy-start | bytes 61444
  79.2 31.6 %collective-permute-start.5 = (bf16[640,1280]{1,0:T(8,128)(2,1)}, bf16[640,1280]{1,0:T(8,128)(2,1)}, u32[]{:S(2)}, u32[]{:S(2)}) collective-permute-start(bf16[640,1280]{1,0:T(8,128)(2,1)} %collective-permute-done.4), channel_id=1, source_target_pairs={{0,1},{1,2},{2,3},{3,4},{4,5},{5,6},{6,7},{7,0},{8,9},{9,10},{10,1... | collective-permute-start | bytes 4915208 | tf_op jit(solution)/shard_map/ppermute | solution.py:116
  82.0 65.5 %collective-permute-start.2 = (bf16[2,4,1,32,5120]{4,3,2,1,0:T(8,128)(2,1)}, bf16[2,4,1,32,5120]{4,3,2,1,0:T(8,128)(2,1)}, u32[]{:S(2)}, u32[]{:S(2)}) collective-permute-start(bf16[2,4,1,32,5120]{4,3,2,1,0:T(8,128)(2,1)} %get-tuple-element.7), channel_id=1, source_target_pairs={{0,1},{1,2},{2,3},{3,4},{4,5},{5,6},{6,7},{8,9},{9,10},{10,11},{11... | collective-permute-start | bytes 7864328 | tf_op jit(solution)/shard_map/ppermute | solution.py:12
  87.0 60.5 %collective-permute-start.3 = (bf16[2,4,1,32,5120]{4,3,2,1,0:T(8,128)(2,1)}, bf16[2,4,1,32,5120]{4,3,2,1,0:T(8,128)(2,1)}, u32[]{:S(2)}, u32[]{:S(2)}) collective-permute-start(bf16[2,4,1,32,5120]{4,3,2,1,0:T(8,128)(2,1)} %get-tuple-element.8), channel_id=1, source_target_pairs={{1,0},{2,1},{3,2},{4,3},{5,4},{6,5},{7,6},{9,8},{10,9},{11,10},{12... | collective-permute-start | bytes 7864328 | tf_op jit(solution)/shard_map/ppermute | solution.py:12
  110.7 36.8 %collective-permute-start.6 = (bf16[640,1280]{1,0:T(8,128)(2,1)}, bf16[640,1280]{1,0:T(8,128)(2,1)}, u32[]{:S(2)}, u32[]{:S(2)}) collective-permute-start(bf16[640,1280]{1,0:T(8,128)(2,1)} %collective-permute-done.5), channel_id=1, source_target_pairs={{0,1},{1,2},{2,3},{3,4},{4,5},{5,6},{6,7},{7,0},{8,9},{9,10},{10,1... | collective-permute-start | bytes 4915208 | tf_op jit(solution)/shard_map/ppermute | solution.py:116
  147.5 25.9 %collective-permute-start.7 = (bf16[640,1280]{1,0:T(8,128)(2,1)}, bf16[640,1280]{1,0:T(8,128)(2,1)}, u32[]{:S(2)}, u32[]{:S(2)}) collective-permute-start(bf16[640,1280]{1,0:T(8,128)(2,1)} %collective-permute-done.6), channel_id=1, source_target_pairs={{0,1},{1,2},{2,3},{3,4},{4,5},{5,6},{6,7},{7,0},{8,9},{9,10},{10,1... | collective-permute-start | bytes 4915208 | tf_op jit(solution)/shard_map/ppermute | solution.py:116
  165.5 6.4 %copy-start = (bf16[1,4,4,32,5120]{4,3,2,1,0:T(8,128)(2,1)S(1)}, bf16[1,4,4,32,5120]{4,3,2,1,0:T(8,128)(2,1)}, u32[]{:S(2)}) copy-start(bf16[1,4,4,32,5120]{4,3,2,1,0:T(8,128)(2,1)} %get-tuple-element.6) | copy-start | bytes 15728644
  172.0 1.7 copy-start.3
  172.0 1.7 copy-start.6
  172.0 1.7 copy-start.7
  172.0 1.8 copy-start.8
  173.4 22.8 %collective-permute-start.8 = (bf16[640,1280]{1,0:T(8,128)(2,1)}, bf16[640,1280]{1,0:T(8,128)(2,1)S(1)}, u32[]{:S(2)}, u32[]{:S(2)}) collective-permute-start(bf16[640,1280]{1,0:T(8,128)(2,1)} %collective-permute-done.7), channel_id=1, source_target_pairs={{0,1},{1,2},{2,3},{3,4},{4,5},{5,6},{6,7},{7,0},{8,9},{9,10},{10,1... | collective-permute-start | bytes 4915208 | tf_op jit(solution)/shard_map/ppermute | solution.py:116
  178.4 4.0 %copy-start.2 = (f32[40,128,512]{2,1,0:T(8,128)}, f32[40,128,512]{2,1,0:T(8,128)S(1)}, u32[]{:S(2)}) copy-start(f32[40,128,512]{2,1,0:T(8,128)S(1)} %get-tuple-element.12) | copy-start | bytes 31457284
  196.2 22.3 %collective-permute-start.9 = (bf16[640,1280]{1,0:T(8,128)(2,1)S(1)}, bf16[640,1280]{1,0:T(8,128)(2,1)S(1)}, u32[]{:S(2)}, u32[]{:S(2)}) collective-permute-start(bf16[640,1280]{1,0:T(8,128)(2,1)S(1)} %collective-permute-done.8), channel_id=1, source_target_pairs={{0,1},{1,2},{2,3},{3,4},{4,5},{5,6},{6,7},{7,0},{8,9},{9,10},{10,1... | collective-permute-start | bytes 4915208 | tf_op jit(solution)/shard_map/ppermute | solution.py:116
  218.6 22.4 %collective-permute-start.10 = (bf16[640,1280]{1,0:T(8,128)(2,1)S(1)}, bf16[640,1280]{1,0:T(8,128)(2,1)}, u32[]{:S(2)}, u32[]{:S(2)}) collective-permute-start(bf16[640,1280]{1,0:T(8,128)(2,1)S(1)} %collective-permute-done.9), channel_id=1, source_target_pairs={{0,1},{1,2},{2,3},{3,4},{4,5},{5,6},{6,7},{7,0},{8,9},{9,10},{10,1... | collective-permute-start | bytes 4915208 | tf_op jit(solution)/shard_map/ppermute | solution.py:116
  316.5 4.2 %copy-start.5 = (f32[5120]{0:T(1024)S(1)}, f32[5120]{0:T(1024)}, u32[]{:S(2)}) copy-start(f32[5120]{0:T(1024)} %param.21) | copy-start | bytes 61444
Sparse Core Ops, SparseCore 0:
  206.2 61.4 all-gather.1
